TPU v7x, 32 devices: a whole 2x2x4 slice. The times are simulated.
32 devices in a mesh: dp: 16 (over z, y, x), outer: 2 (over core).
Axes of the slice: x: 2, y: 2, z: 4, core: 2. Of those that a mesh axis runs over, the one named last changes fastest.
Arguments:
- gradient: float32 [32, 131072], P(('dp', 'outer')), may hold values from -6 to 6
- residual: float32 [32, 131072], P(('dp', 'outer')), may hold values from -6 to 6
- indices: int32 [32, 512], P(('dp', 'outer')), may hold values from 0 to 131071, as said below
- params: float32 [131072], replicated, may hold values from -6 to 6
Outputs:
- new_params: float32 [131072], replicated
- new_residual: float32 [32, 131072], P(('dp', 'outer'))
Inputs may be any that keep to these rules, and one draw needn't show every extreme that they name: Within each worker's row the 512 indices are distinct and increasing: index j lies in [j * 256, (j + 1) * 256). Different workers often pick the same coordinate.
All inputs are finite; a program needn't handle non-finite values.
Results may differ from a plain program's by a relative error of at most 0.0003.
Values sent between devices are 32-bit elements.
A program may use at most 64 MiB of HBM per device.

v0:
```python
import jax
import jax.numpy as jnp
from jax import lax
from jax.sharding import PartitionSpec as P

step_size = 0.5


def over_all(section, axis, dim, step, start):
    def gathered(part):
        return lax.all_gather(part, axis, axis=dim, tiled=True)

    return step(start, jax.tree.map(gathered, section), jnp.int32(0))


def add_pairs(carried, pieces, offset_at):
    return carried.at[pieces[1]].add(pieces[0])


def shards(gradient, residual, indices, params):
    accumulated = gradient[0] + residual[0]
    positions = indices[0]
    values_sent = accumulated[positions]
    new_residual = accumulated.at[positions].set(jnp.float32(0.0))[None, :]
    empty = jnp.zeros((accumulated.shape[0],), jnp.float32)
    total = over_all((values_sent, positions), ("dp", "outer"), 0, add_pairs, empty)
    new_params = params - step_size * total
    return (new_params, new_residual)


def solution(mesh):
    placed = (P(("dp", "outer"), None), P(("dp", "outer"), None), P(("dp", "outer"), None), P())
    return jax.shard_map(
        shards,
        mesh=mesh,
        in_specs=placed,
        out_specs=(P(), P(("dp", "outer"), None)),
        check_vma=False,
    )
```

profile of v0, /device:TPU:0, one launch (start us, length us, event | category | flops | bytes accessed | tf_op | source)
XLA Modules:
  0.0 185.6 jit_solution(16264902432513575408)
XLA Ops:
  0.6 0.7 compare_select_fusion.1
  1.3 0.0 copy-start.2
  1.3 0.7 copy-done.2
  2.0 43.4 %all-gather = s32[1,16384]{1,0:T(1,128)S(1)} all-gather(s32[1,512]{1,0:T(1,128)S(1)} %copy-done.2), channel_id=2, replica_groups=mesh['dp'=16,'outer'=2] {'dp','outer'}, dimensions={1}, use_global_device_ids=true | all-gather | bytes 67584 | tf_op jit(solution)/shard_map/all_gather | solution.py:11
  45.4 1.7 add.27
  47.2 3.1 %gather_fusion = f32[512]{0:T(512)S(1)} fusion(f32[131072]{0:T(1024)S(1)} %bitcast.9, s32[1024]{0:T(1024)S(1)} %pad_clamp_fusion), kind=kCustom, calls=%fused_computation | custom fusion | bytes 6144 | tf_op jit(solution)/shard_map/gather | solution.py:23
  50.4 2.7 %scatter_fusion = f32[131072]{0:T(1024)S(1)} fusion(f32[131072]{0:T(1024)S(1)} %bitcast.10, s32[512]{0:T(512)S(1)} %bitcast.15, f32[512]{0:T(512)S(1)} %broadcast.22), kind=kCustom, calls=%fused_computation.2 | custom fusion | bytes 8192 | tf_op jit(solution)/shard_map/scatter | solution.py:24
  53.0 0.0 copy-start
  53.1 0.0 copy-start.1
  53.1 36.9 %all-gather.2 = f32[32,1,512]{2,1,0:T(1,128)S(1)} all-gather(f32[1,1,512]{2,1,0:T(1,128)S(1)} %bitcast.16), channel_id=3, replica_groups=mesh['dp'=16,'outer'=2] {'dp','outer'}, dimensions={0}, use_global_device_ids=true | all-gather | bytes 67584 | tf_op jit(solution)/shard_map/all_gather | solution.py:11
  90.0 94.7 %scatter_custom_fusion = f32[131072]{0:T(1024)S(1)} fusion(s32[16384]{0:T(1024)S(1)} %compare_select_fusion, f32[16384]{0:T(1024)S(1)} %bitcast.13, f32[]{:T(128)} %constant.4.clone.1), kind=kCustom, calls=%fused_computation.4 | custom fusion | flops 16384 | bytes 524292 | tf_op jit(solution)/shard_map/scatter-add | solution.py:17
  184.7 0.0 copy-done.1
  184.7 0.8 multiply_subtract_fusion
  185.6 0.0 copy-done
  (3 shorter events, 0.0 us)
Async XLA Ops:
  1.3 0.7 copy-start.2
  53.0 132.5 %copy-start = (f32[131072]{0:T(1024)}, f32[131072]{0:T(1024)S(1)}, u32[]{:S(2)}) copy-start(f32[131072]{0:T(1024)S(1)} %scatter_fusion) | copy-start | bytes 1572868
  53.1 131.6 %copy-start.1 = (f32[131072]{0:T(1024)S(1)}, f32[131072]{0:T(1024)}, u32[]{:S(2)}) copy-start(f32[131072]{0:T(1024)} %param.7) | copy-start | bytes 1572868
where the time goes:
time: 186 us
  other arithmetic  98 us (53%)
  blocking collectives  80.4 us (43%)
  local copies, waits for them, and re-layouts  6.52 us (4%)
    scatter-add x1, other arithmetic, add_pairs(): return carried.at[pieces[1]].add(pieces[0])  94.7 us
    all_gather x2, blocking collectives, gathered(): return lax.all_gather(part, axis, axis=dim, tiled=True)  80.4 us

commit v1 on v0

v1 whole, which is shorter than its diff:
```python
import functools

import jax
import jax.numpy as jnp
from jax import lax
from jax.experimental import pallas as pl
from jax.experimental.pallas import tpu as pltpu
from jax.sharding import PartitionSpec as P

MESH = pl.DeviceIdType.MESH
step_size = 0.5
LANES = 128
GROUPS = 4
CHUNK = 8
STRIP = 64


def kernel(n, outer, gradient, residual, indices, total, kept,
           grad_v, resid_v, index_v, pairs, turned, partial,
           in_sem, send_sem, recv_sem):
    tiles = indices.shape[0]
    block = gradient.shape[0] // tiles
    halves = block // LANES
    me = lax.axis_index("dp") * outer + lax.axis_index("outer")

    def at(worker):
        return (worker // outer, lax.rem(worker, outer))

    loads = [pltpu.make_async_copy(indices, index_v, in_sem.at[2 * tiles])]
    for t in range(tiles):
        rows = pl.ds(t * block, block)
        loads.append(pltpu.make_async_copy(gradient.at[rows], grad_v.at[rows], in_sem.at[2 * t]))
        loads.append(pltpu.make_async_copy(residual.at[rows], resid_v.at[rows], in_sem.at[2 * t + 1]))
    for load in loads:
        load.start()

    barrier = pltpu.get_barrier_semaphore()

    def greet(k, carry):
        pl.semaphore_signal(barrier, inc=1, device_id=at(lax.rem(me + k, n)), device_id_type=MESH)
        return carry

    lax.fori_loop(1, n, greet, 0)

    loads[0].wait()
    blocks = (lax.broadcasted_iota(jnp.int32, index_v.shape, 0) * LANES
              + lax.broadcasted_iota(jnp.int32, index_v.shape, 1))
    offsets = (index_v[...] - blocks * (halves * LANES)).astype(jnp.float32)
    row_at = lax.broadcasted_iota(jnp.int32, (LANES, LANES), 0).astype(jnp.float32)

    def chosen(t, h):
        return offsets[t:t + 1, :] - jnp.float32(h * LANES) == row_at

    sent = []
    for t in range(tiles):
        loads[1 + 2 * t].wait()
        loads[2 + 2 * t].wait()
        mine = jnp.zeros((1, LANES), jnp.float32)
        for h in range(halves):
            rows = pl.ds(t * block + h, LANES, stride=halves)
            flipped = (grad_v[rows, :] + resid_v[rows, :]).T
            turned[h * LANES:(h + 1) * LANES, t * LANES:(t + 1) * LANES] = flipped
            mine += jnp.sum(jnp.where(chosen(t, h), flipped, 0.0), axis=0, keepdims=True)
        sent.append(mine)
    pairs[me] = jnp.concatenate(sent + [offsets], axis=0)

    pl.semaphore_wait(barrier, n - 1)

    def copy_to(worker):
        return pltpu.make_async_remote_copy(
            src_ref=pairs.at[me], dst_ref=pairs.at[me],
            send_sem=send_sem.at[worker], recv_sem=recv_sem.at[me],
            device_id=at(worker), device_id_type=MESH)

    def copy_from(worker):
        return pltpu.make_async_remote_copy(
            src_ref=pairs.at[me], dst_ref=pairs.at[worker],
            send_sem=send_sem.at[worker], recv_sem=recv_sem.at[worker],
            device_id=at(worker), device_id_type=MESH)

    def send(k, carry):
        worker = lax.rem(me + n // 2 + k, n)

        @pl.when(worker != me)
        def _():
            copy_to(worker).start()

        return carry

    lax.fori_loop(0, n, send, 0)

    for t in range(tiles):
        for h in range(halves):
            flipped = turned[h * LANES:(h + 1) * LANES, t * LANES:(t + 1) * LANES]
            rows = pl.ds(t * block + h, LANES, stride=halves)
            kept[rows, :] = jnp.where(chosen(t, h), 0.0, flipped).T

    size = n // GROUPS
    strip_at = lax.broadcasted_iota(jnp.int32, (STRIP, LANES), 0).astype(jnp.float32)
    my_group = me // size

    def add_group(i, carry):
        away = jnp.where(i == 2, 3, jnp.where(i == 3, 2, i))
        group = lax.rem(my_group + away, GROUPS)

        def arrived(k, carry):
            worker = group * size + k

            @pl.when(worker != me)
            def _():
                copy_from(worker).wait_recv()

            return carry

        lax.fori_loop(0, size, arrived, 0)
        for first in range(0, size, CHUNK):
            many = min(CHUNK, size - first)
            for t in range(tiles):
                lanes = slice(t * LANES, (t + 1) * LANES)
                for s in range(0, halves * LANES, STRIP):
                    strip = (group, slice(s, s + STRIP), lanes)
                    added = None
                    for k in range(many):
                        pair = pairs.at[group * size + first + k]
                        hit = pair[tiles + t:tiles + t + 1, :] - jnp.float32(s) == strip_at
                        value = jnp.where(hit, pair[t:t + 1, :], 0.0)
                        added = value if added is None else added + value
                    if first:
                        added = added + partial[strip]
                    partial[strip] = added
        return carry

    lax.fori_loop(0, GROUPS, add_group, 0)

    for t in range(tiles):
        for h in range(halves):
            piece = (slice(h * LANES, (h + 1) * LANES), slice(t * LANES, (t + 1) * LANES))
            summed = partial[(0,) + piece]
            for group in range(1, GROUPS):
                summed = summed + partial[(group,) + piece]
            rows = pl.ds(t * block + h, LANES, stride=halves)
            total[rows, :] = summed.T

    def sent_off(k, carry):
        copy_to(lax.rem(me + k, n)).wait_send()
        return carry

    lax.fori_loop(1, n, sent_off, 0)


def shards(n, outer, gradient, residual, indices, params):
    width, keep = gradient.shape[1], indices.shape[1]
    tiles, block = keep // LANES, width // keep
    long = (width // LANES, LANES)
    any_space = pl.BlockSpec(memory_space=pl.ANY)
    vmem = pl.BlockSpec(memory_space=pltpu.VMEM)
    total, kept = pl.pallas_call(
        functools.partial(kernel, n, outer),
        out_shape=[jax.ShapeDtypeStruct(long, jnp.float32)] * 2,
        in_specs=[any_space] * 3,
        out_specs=[vmem] * 2,
        scratch_shapes=[
            pltpu.VMEM(long, jnp.float32),
            pltpu.VMEM(long, jnp.float32),
            pltpu.VMEM((tiles, LANES), jnp.int32),
            pltpu.VMEM((n, 2 * tiles, LANES), jnp.float32),
            pltpu.VMEM((block, keep), jnp.float32),
            pltpu.VMEM((GROUPS, block, keep), jnp.float32),
            pltpu.SemaphoreType.DMA((2 * tiles + 1,)),
            pltpu.SemaphoreType.DMA((n,)),
            pltpu.SemaphoreType.DMA((n,)),
        ],
        compiler_params=pltpu.CompilerParams(collective_id=0, has_side_effects=True),
    )(gradient.reshape(long), residual.reshape(long), indices.reshape(tiles, LANES))
    new_params = params - step_size * total.reshape(width)
    return new_params, kept.reshape(1, width)


def solution(mesh):
    outer = mesh.shape["outer"]
    n = mesh.shape["dp"] * outer
    placed = (P(("dp", "outer"), None), P(("dp", "outer"), None), P(("dp", "outer"), None), P())
    return jax.shard_map(
        functools.partial(shards, n, outer),
        mesh=mesh,
        in_specs=placed,
        out_specs=(P(), P(("dp", "outer"), None)),
        check_vma=False,
    )
```

time: 186 us -> 17.8 us (0.10)
  other arithmetic: 98 us -> 1.94 us
  blocking collectives: 80.4 us -> 0 us
  Pallas kernels: 0 us -> 14.3 us
  local copies, waits for them, and re-layouts: 6.52 us -> 0.8 us
    scatter-add x1 -> x0, other arithmetic: 94.7 us -> none  [add_pairs(): return carried.at[pieces[1]].add(pieces[0])]
    all_gather x2 -> x0, blocking collectives: 80.4 us -> none  [gathered(): return lax.all_gather(part, axis, axis=dim, tiled=True)]
    pallas_call x0 -> x1, Pallas kernels: none -> 14.3 us  [shards(): pl.pallas_call(functools.partial(kernel, n, outer), out_shape=[jax.ShapeD...]
    gather x1 -> x0, local copies, waits for them, and re-layouts: 3.14 us -> none  [shards(): values_sent = accumulated[positions]]
    scatter x1 -> x0, local copies, waits for them, and re-layouts: 2.69 us -> none  [shards(): new_residual = accumulated.at[positions].set(jnp.float32(0.0))[None, :]]
where the time goes in v1:
time: 17.8 us; the launch traced here: 17.7 us
  Pallas kernels  14.3 us (80%)
  other arithmetic  1.94 us (11%)
  local copies, waits for them, and re-layouts  0.8 us (4%)
  between operations  0.66 us (4%)
    pallas_call x1, Pallas kernels, shards(): pl.pallas_call(functools.partial(kernel, n, outer), out_shape=[jax.ShapeD...  14.3 us
    sub x1, other arithmetic, shards(): new_params = params - step_size * total.reshape(width)  1.94 us
    unnamed x5, local copies, waits for them, and re-layouts  0.8 us

profile of v1, /device:TPU:0, one launch (start us, length us, event | category | flops | bytes accessed | tf_op | source)
XLA Modules:
  0.0 17.7 jit_solution(254164581370781285)
XLA Ops:
  0.6 0.0 copy-start
  0.6 14.3 %shard_map.59 = (f32[1024,128]{1,0:T(8,128)}, f32[1024,128]{1,0:T(8,128)}) custom-call(f32[1024,128]{1,0:T(8,128)} %bitcast.6, f32[1024,128]{1,0:T(8,128)} %bitcast.7, s32[4,128]{1,0:T(4,128)} %bitcast.9), custom_call_target="tpu_custom_call" | custom-call | tf_op jit(solution)/shard_map/pallas_call | solution.py:157
  14.9 0.0 copy-done
  14.9 0.0 copy-start.1
  14.9 1.9 %bitcast_subtract_fusion = f32[131072]{0:T(1024)} fusion(f32[131072]{0:T(1024)S(1)} %copy-done, f32[1024,128]{1,0:T(8,128)} %get-tuple-element.4), kind=kLoop, calls=%fused_computation | loop fusion | flops 262144 | bytes 1572864 | tf_op jit(solution)/shard_map/sub | solution.py:175
  16.9 0.0 copy-done.1
  16.9 0.8 %copy.7 = f32[1,131072]{1,0:T(1,128)} copy(f32[1,131072]{1,0:T(1,128)S(1)} %bitcast.8) | data formatting | bytes 1048576
Async XLA Ops:
  0.6 14.3 %copy-start = (f32[131072]{0:T(1024)S(1)}, f32[131072]{0:T(1024)}, u32[]{:S(2)}) copy-start(f32[131072]{0:T(1024)} %param.7) | copy-start | bytes 1572868
  14.9 2.0 %copy-start.1 = (f32[1024,128]{1,0:T(8,128)S(1)}, f32[1024,128]{1,0:T(8,128)}, u32[]{:S(2)}) copy-start(f32[1024,128]{1,0:T(8,128)} %get-tuple-element.5) | copy-start | bytes 1572868
